TPU v7x, 32 devices: a whole 2x2x4 slice. The times are simulated.
32 devices in a mesh: row: 4 (over y, core), col: 8 (over z, x).
Axes of the slice: x: 2, y: 2, z: 4, core: 2. Of those that a mesh axis runs over, the one named last changes fastest.
Arguments:
- l_saved: bfloat16 [16, 4, 256, 8, 256], P(None, 'row', None, 'col'), as said below
- l_grad: bfloat16 [16, 4, 256, 8, 256], P(None, 'row', None, 'col'), as said below
Outputs:
- grad_out: float32 [16, 4, 256, 8, 256], P(None, 'row', None, 'col')
Inputs may be any that keep to these rules, and one draw needn't show every extreme that they name: Read as one matrix of 16384 rows, l_saved is lower triangular with its diagonal between 1 and 2. Read as one matrix, l_grad is zero above the diagonal.
All inputs are finite; a program needn't handle non-finite values.
Results may differ from a plain program's by a relative error of at most 0.0003.
Values may be sent and summed in bfloat16 or wider, within the bound.
A program may use at most 64 MiB of HBM per device.

v0:
```python
import jax
import jax.numpy as jnp
from jax import lax
from jax.sharding import PartitionSpec as P

F32 = jnp.float32
BF16 = jnp.bfloat16
HIGH3 = lax.Precision.HIGH


def dot3(a, b, ca=1, cb=0):
    return lax.dot_general(
        a, b, (((ca,), (cb,)), ((), ())), precision=HIGH3, preferred_element_type=F32
    )


def bdot(a, b):
    return lax.dot_general(
        a, b, (((2,), (1,)), ((0,), (0,))), precision=HIGH3, preferred_element_type=F32
    )


def inverse_pair(tiles):
    tile = tiles.shape[-1]
    rows = lax.broadcasted_iota(jnp.int32, (tile, tile), 0)
    cols = lax.broadcasted_iota(jnp.int32, (tile, tile), 1)
    eye = (rows == cols).astype(F32)
    recip = 1.0 / jnp.sum(tiles * eye, axis=2)
    inv = eye * recip[:, None, :]
    size = 1
    while size < tile:
        off = (rows // size % 2 == 1) & (cols // size == rows // size - 1)
        part = jnp.where(off, tiles, 0.0)
        if size == 1:
            inv = inv - recip[:, :, None] * part * recip[:, None, :]
        else:
            inv = inv - bdot(inv, bdot(part, inv))
        size *= 2
    return inv


def per_device(l_saved, l_grad):
    rows_here, tile = (l_saved.shape[0], l_saved.shape[2])
    n_row = lax.axis_size("row")
    n_col = lax.axis_size("col")
    factor = l_saved.reshape(rows_here, tile, tile)
    grad = l_grad.reshape(rows_here, tile, tile)
    my_row = lax.axis_index("row")
    my_col = lax.axis_index("col")
    assert n_col % n_row == 0
    first = n_col // n_row
    loc = first - 1
    lo, hi = (n_col - 2, n_col - 1)
    l_dk = lax.all_gather(factor[loc], "row")[n_row - 2 :].reshape(2 * tile, tile)
    mine = jnp.concatenate([l_dk, grad[first:].reshape(-1, tile)], 0)
    zero = jnp.zeros_like(mine)
    both = jnp.concatenate(
        [jnp.where(my_col == lo, mine, zero), jnp.where(my_col == hi, mine, zero)], 1
    )
    both = lax.psum(both, "col")
    l_dd = both[: 2 * tile].astype(F32)
    g_d = both[2 * tile :]
    l66, l76, l77 = (l_dd[:tile, :tile], l_dd[tile:, :tile], l_dd[tile:, tile:])
    inv = inverse_pair(jnp.stack([l66, l77]))
    w76 = -dot3(inv[1], dot3(l76, inv[0]))
    w = jnp.concatenate(
        [jnp.concatenate([inv[0], jnp.zeros_like(w76)], 1), jnp.concatenate([w76, inv[1]], 1)], 0
    )
    below_l = factor[first:].reshape(-1, tile)
    h = lax.dot_general(g_d, below_l, (((0,), (0,)), ((), ())), preferred_element_type=F32)
    t = dot3(w, lax.psum(h, "row"), 0, 0)
    fresh = grad[loc].astype(F32)
    g_dk = lax.all_gather(grad[loc], "row")[n_row - 2 :].reshape(2 * tile, tile).astype(F32)
    q_mine = g_dk - t
    z2 = jnp.zeros_like(q_mine)
    q = lax.psum(
        jnp.concatenate(
            [jnp.where(my_col == lo, q_mine, z2), jnp.where(my_col == hi, q_mine, z2)], 1
        ),
        "col",
    )
    eye2 = jnp.eye(2 * tile, dtype=F32)
    q = jnp.tril(q)
    m = dot3(l_dd, q, 0, 0)
    phi = jnp.tril(m) - 0.5 * m * eye2
    half = dot3(dot3(w, phi, 0, 0), w)
    s = half + half.T
    out_dd = jnp.tril(s) - 0.5 * s * eye2
    right = my_col >= lo
    w_mine = jnp.where(my_col == lo, w[:, :tile], w[:, tile:])
    x = jnp.where(right, -w_mine, dot3(w, l_dk.astype(F32)))
    x_hi = lax.reduce_precision(x, 8, 7)
    x_lo = (x - x_hi).astype(BF16)
    x_hi = x_hi.astype(BF16)
    prod = jnp.dot(g_d, x_hi, preferred_element_type=F32) + jnp.dot(
        g_d, x_lo, preferred_element_type=F32
    )
    base = jnp.where(right, jnp.zeros((), BF16), grad[first:]).astype(F32)
    low = base - prod.reshape(-1, tile, tile)
    at_lo = my_row == n_row - 2
    s_row = jnp.where(at_lo, s[:tile], s[tile:])
    t_row = jnp.where(at_lo, t[:tile], t[tile:])
    own = fresh - (t_row + dot3(s_row, l_dk.astype(F32)))
    d_row = jnp.where(at_lo, out_dd[:tile], out_dd[tile:])
    d_own = jnp.where(my_col == lo, d_row[:, :tile], d_row[:, tile:])
    in_panel = my_row >= n_row - 2
    zt = jnp.zeros_like(fresh)
    own = jnp.where(in_panel, jnp.where(right, d_own, own), jnp.where(right, zt, fresh))
    upper = jnp.where(right, jnp.zeros((), BF16), grad[:loc]).astype(F32)
    out = jnp.concatenate([upper, own[None], low], 0)
    return out.reshape(l_grad.shape)


def solution(mesh):
    spec = P(None, "row", None, "col", None)
    return jax.shard_map(
        per_device, mesh=mesh, in_specs=(spec, spec), out_specs=spec, check_vma=False
    )
```

profile of v0, /device:TPU:0, one launch (start us, length us, event | category | flops | bytes accessed | tf_op | source)
XLA Modules:
  0.0 323.6 jit_solution(8879946724786427271)
XLA Ops:
  6.5 0.9 slice.87
  7.5 8.7 %all-gather = bf16[4,1,256,1,256]{4,2,3,1,0:T(8,128)(2,1)S(1)} all-gather(bf16[1,1,256,1,256]{4,2,3,1,0:T(8,128)(2,1)S(1)} %slice.87), channel_id=2, replica_groups=mesh['row'=4,'col'=8] {'row'}, dimensions={0}, use_global_device_ids=true | all-gather | bytes 655360 | tf_op jit(solution)/shard_map/all_gather | solution.py:54
  16.2 1.7 slice.115
  18.6 2.3 pad_maximum_fusion
  21.0 1.5 copy-done.3
  23.2 7.3 %all-gather.1 = bf16[4,1,256,1,256]{4,2,3,1,0:T(8,128)(2,1)S(1)} all-gather(bf16[1,1,256,1,256]{4,2,3,1,0:T(8,128)(2,1)S(1)} %get-tuple-element.8), channel_id=3, replica_groups=mesh['row'=4,'col'=8] {'row'}, dimensions={0}, use_global_device_ids=true | all-gather | bytes 655360 | tf_op jit(solution)/shard_map/all_gather | solution.py:73
  30.5 0.7 slice.122
  32.9 145.4 %all-reduce.5.cloned.1.call-done = bf16[4096,512]{1,0:T(8,128)(2,1)} async-done(((bf16[4096,512]{1,0:T(8,128)(2,1)}), bf16[4096,512]{1,0:T(8,128)(2,1)}) %all-reduce.5.cloned.1.call-update) | async-done | bytes 4194320 | tf_op jit(solution)/shard_map/psum | solution.py:60
  178.3 1.2 slice_convert_fusion
  186.8 1.9 fusion.3
  189.1 1.4 convolution_select_fusion
  190.5 30.8 %all-reduce.7.cloned.1.call-done = f32[512,256]{1,0:T(8,128)} async-done(((f32[512,256]{1,0:T(8,128)}), f32[512,256]{1,0:T(8,128)}) %all-reduce.7.cloned.1.call-update) | async-done | bytes 524304 | tf_op jit(solution)/shard_map/psum | solution.py:71
  221.3 2.7 fusion.40
  224.0 1.2 pad_maximum_fusion.3
  225.2 3.3 %fusion.1 = f32[3584,256]{1,0:T(8,128)S(1)} fusion(bf16[4096,512]{1,0:T(8,128)(2,1)} %all-reduce.5.cloned.1.call-done, f32[512,256]{1,0:T(8,128)S(1)} %convolution_select_fusion), kind=kOutput, calls=%fused_computation.5 | convolution fusion | flops 939786240 | bytes 7864320 | tf_op jit(solution)/shard_map/dot_general | solution.py:95
  228.5 1.1 convolution_add_fusion
  229.7 2.3 convert_subtract_fusion
  231.9 71.8 %all-reduce.9.cloned.1.call-done = f32[512,512]{1,0:T(8,128)} async-done(((f32[512,512]{1,0:T(8,128)}), f32[512,512]{1,0:T(8,128)}) %all-reduce.9.cloned.1.call-update) | async-done | bytes 1048592 | tf_op jit(solution)/shard_map/psum | solution.py:76
  303.7 2.2 fusion.14
  305.9 1.0 fusion.9
  307.0 2.0 fusion.113
  309.0 1.3 copy.12
  310.3 1.6 select_subtract_fusion
  313.2 3.9 %reshape.79 = f32[16,1,256,1,256]{4,3,2,1,0:T(1,128)} reshape(f32[16,256,256]{2,1,0:T(8,128)S(1)} %pad_maximum_fusion.1) | data formatting | bytes 8388608 | tf_op jit(solution)/shard_map/reshape | solution.py:111
  (77 shorter events, 11.8 us)
Async XLA Ops:
  6.5 171.8 %all-reduce.5.cloned.1.call-start = ((), (), s32[]{:S(2)}) async-start(), calls=%async_computation | async-start | bytes 8388608 | tf_op jit(solution)/shard_map/psum | solution.py:60
  16.2 2.4 copy-start.6
  20.9 1.6 copy-start.3
  20.9 200.4 %all-reduce.7.cloned.1.call-start = ((), (), s32[]{:S(2)}) async-start(), calls=%async_computation.1 | async-start | bytes 1048576 | tf_op jit(solution)/shard_map/psum | solution.py:71
  183.9 2.2 copy-start
  184.3 2.5 slice-start
  186.1 119.8 %copy-start.4 = (f32[256,256]{1,0:T(8,128)}, f32[256,256]{1,0:T(8,128)S(1)}, u32[]{:S(2)}) copy-start(f32[256,256]{1,0:T(8,128)S(1)} %get-tuple-element.15) | copy-start | bytes 786436
  186.1 119.8 %copy-start.5 = (f32[256,256]{1,0:T(8,128)}, f32[256,256]{1,0:T(8,128)S(1)}, u32[]{:S(2)}) copy-start(f32[256,256]{1,0:T(8,128)S(1)} %get-tuple-element.16) | copy-start | bytes 786436
  188.8 115.0 %all-reduce.9.cloned.1.call-start = ((), (), s32[]{:S(2)}) async-start(), calls=%async_computation.2 | async-start | bytes 2097152 | tf_op jit(solution)/shard_map/psum | solution.py:76
  225.2 3.3 %copy-start.1 = (bf16[4096,512]{1,0:T(8,128)(2,1)S(1)}, bf16[4096,512]{1,0:T(8,128)(2,1)}, u32[]{:S(2)}) copy-start(bf16[4096,512]{1,0:T(8,128)(2,1)} %all-reduce.5.cloned.1.call-done) | copy-start | bytes 12582916
  309.0 3.1 copy-start.7
  310.3 1.7 copy-start.9
  310.3 2.5 copy-start.2
  310.3 2.5 copy-start.8
Sparse Core Ops, SparseCore 0:
  21.1 157.1 all-reduce.4
  188.9 32.3 all-reduce.6
  225.3 78.3 all-reduce.8
where the time goes:
time: 324 us
  waiting for transfers between devices  248 us (77%)
  matrix products  22.3 us (7%)
  blocking collectives  15.9 us (5%)
  between operations  13.6 us (4%)
  other arithmetic  12.1 us (4%)
  local copies, waits for them, and re-layouts  11.3 us (3%)
    psum x1, waiting for transfers between devices, per_device(): both = lax.psum(both, 'col')  145 us
    psum x1, waiting for transfers between devices, per_device(): lax.psum(jnp.concatenate([jnp.where(my_col == lo, q_mine, z2), jnp.where(...  71.8 us
    psum x1, waiting for transfers between devices, per_device(): t = dot3(w, lax.psum(h, 'row'), 0, 0)  30.8 us
    dot_general x8, matrix products, dot3(): lax.dot_general(a, b, (((ca,), (cb,)), ((), ())), precision=HIGH3, prefer...  10.1 us
    all_gather x1, blocking collectives, per_device(): lax.all_gather(factor[loc], 'row')[n_row - 2:].reshape(2 * tile, tile)  8.68 us
    all_gather x1, blocking collectives, per_device(): lax.all_gather(grad[loc], 'row')[n_row - 2:].reshape(2 * tile, tile)  7.26 us
  transfers between devices with their start and end apart: 3, of which 3 were waited for; matrix products, arithmetic and copies ran while one was open for 3% of the time, Pallas kernels for 0%

commit v1 on v0

--- a/solution.py
+++ b/solution.py
@@ -1,3 +1,4 @@
+import functools
 import jax
 import jax.numpy as jnp
 from jax import lax
@@ -6,6 +7,15 @@
 F32 = jnp.float32
 BF16 = jnp.bfloat16
 HIGH3 = lax.Precision.HIGH
+
+
+def joints_time(u_in, axis_tag):
+    z1 = lax.all_gather(u_in, axis_tag)
+    aux = jnp.sum(z1, axis=0)
+    return aux
+
+
+cut_the_outputs = functools.partial(joints_time, axis_tag="row")
 
 
 def dot3(a, b, ca=1, cb=0):
@@ -68,7 +78,7 @@
     )
     below_l = factor[first:].reshape(-1, tile)
     h = lax.dot_general(g_d, below_l, (((0,), (0,)), ((), ())), preferred_element_type=F32)
-    t = dot3(w, lax.psum(h, "row"), 0, 0)
+    t = dot3(w, cut_the_outputs(h), 0, 0)
     fresh = grad[loc].astype(F32)
     g_dk = lax.all_gather(grad[loc], "row")[n_row - 2 :].reshape(2 * tile, tile).astype(F32)
     q_mine = g_dk - t

time: 324 us -> 312 us (0.963)
  waiting for transfers between devices: 248 us -> 233 us
    psum x1 -> x0, waiting for transfers between devices: 30.8 us -> none  [per_device(): t = dot3(w, lax.psum(h, 'row'), 0, 0)]
    all_gather x0 -> x1, waiting for transfers between devices: none -> 16.2 us  [joints_time(): z1 = lax.all_gather(u_in, axis_tag)]
  transfers between devices with their start and end apart: 3 -> 3, of which waited for: 3 -> 3; matrix products, arithmetic and copies ran while one was open for 3% -> 5% of each run, Pallas kernels for 0% -> 0%
where the time goes in v1:
time: 312 us
  waiting for transfers between devices  233 us (75%)
  matrix products  22.2 us (7%)
  blocking collectives  15.9 us (5%)
  other arithmetic  14.7 us (5%)
  between operations  13.6 us (4%)
  local copies, waits for them, and re-layouts  11.8 us (4%)
    psum x1, waiting for transfers between devices, per_device(): both = lax.psum(both, 'col')  145 us
    psum x1, waiting for transfers between devices, per_device(): lax.psum(jnp.concatenate([jnp.where(my_col == lo, q_mine, z2), jnp.where(...  71.7 us
    all_gather x1, waiting for transfers between devices, joints_time(): z1 = lax.all_gather(u_in, axis_tag)  16.2 us
    dot_general x8, matrix products, dot3(): lax.dot_general(a, b, (((ca,), (cb,)), ((), ())), precision=HIGH3, prefer...  10.1 us
    all_gather x1, blocking collectives, per_device(): lax.all_gather(factor[loc], 'row')[n_row - 2:].reshape(2 * tile, tile)  8.68 us
    all_gather x1, blocking collectives, per_device(): lax.all_gather(grad[loc], 'row')[n_row - 2:].reshape(2 * tile, tile)  7.26 us
  transfers between devices with their start and end apart: 3, of which 3 were waited for; matrix products, arithmetic and copies ran while one was open for 5% of the time, Pallas kernels for 0%

profile of v1, /device:TPU:0, one launch (start us, length us, event | category | flops | bytes accessed | tf_op | source)
XLA Modules:
  0.0 311.9 jit_solution(2861691578025098001)
XLA Ops:
  6.5 0.9 slice.87
  7.5 8.7 %all-gather = bf16[4,1,256,1,256]{4,2,3,1,0:T(8,128)(2,1)S(1)} all-gather(bf16[1,1,256,1,256]{4,2,3,1,0:T(8,128)(2,1)S(1)} %slice.87), channel_id=2, replica_groups=mesh['row'=4,'col'=8] {'row'}, dimensions={0}, use_global_device_ids=true | all-gather | bytes 655360 | tf_op jit(solution)/shard_map/all_gather | solution.py:64
  16.2 1.7 slice.115
  18.6 2.3 pad_maximum_fusion
  21.0 1.5 copy-done.3
  23.2 7.3 %all-gather.1 = bf16[4,1,256,1,256]{4,2,3,1,0:T(8,128)(2,1)S(1)} all-gather(bf16[1,1,256,1,256]{4,2,3,1,0:T(8,128)(2,1)S(1)} %get-tuple-element.8), channel_id=3, replica_groups=mesh['row'=4,'col'=8] {'row'}, dimensions={0}, use_global_device_ids=true | all-gather | bytes 655360 | tf_op jit(solution)/shard_map/all_gather | solution.py:83
  32.9 145.4 %all-reduce.4.cloned.1.call-done = bf16[4096,512]{1,0:T(8,128)(2,1)} async-done(((bf16[4096,512]{1,0:T(8,128)(2,1)}), bf16[4096,512]{1,0:T(8,128)(2,1)}) %all-reduce.4.cloned.1.call-update) | async-done | bytes 4194320 | tf_op jit(solution)/shard_map/psum | solution.py:70
  178.3 1.2 slice_convert_fusion
  183.5 1.9 fusion.3
  188.9 1.1 fusion.99
  191.0 16.2 %all-gather.5.cloned.1.call-done = f32[2048,256]{1,0:T(8,128)} async-done(((f32[512,256]{1,0:T(8,128)}), f32[2048,256]{1,0:T(8,128)}) %all-gather.5.cloned.1.call-update) | async-done | bytes 2097168 | tf_op jit(solution)/shard_map/all_gather | solution.py:13
  207.1 2.6 reduce_sum.19
  209.7 2.7 fusion.40
  212.4 1.1 pad_maximum_fusion.3
  213.6 3.3 %fusion.1 = f32[3584,256]{1,0:T(8,128)S(1)} fusion(bf16[4096,512]{1,0:T(8,128)(2,1)} %all-reduce.4.cloned.1.call-done, f32[512,256]{1,0:T(8,128)S(1)} %convolution_select_fusion), kind=kOutput, calls=%fused_computation.5 | convolution fusion | flops 939786240 | bytes 7864320 | tf_op jit(solution)/shard_map/dot_general | solution.py:105
  216.9 1.1 convolution_add_fusion
  218.1 2.3 convert_subtract_fusion
  220.3 71.7 %all-reduce.6.cloned.1.call-done = f32[512,512]{1,0:T(8,128)} async-done(((f32[512,512]{1,0:T(8,128)}), f32[512,512]{1,0:T(8,128)}) %all-reduce.6.cloned.1.call-update) | async-done | bytes 1048592 | tf_op jit(solution)/shard_map/psum | solution.py:86
  292.0 2.2 fusion.14
  294.2 1.0 fusion.9
  295.3 2.0 fusion.113
  297.3 1.3 copy.12
  298.6 1.6 select_subtract_fusion
  301.5 3.9 %reshape.79 = f32[16,1,256,1,256]{4,3,2,1,0:T(1,128)} reshape(f32[16,256,256]{2,1,0:T(8,128)S(1)} %pad_maximum_fusion.1) | data formatting | bytes 8388608 | tf_op jit(solution)/shard_map/reshape | solution.py:121
  (80 shorter events, 13.2 us)
Async XLA Ops:
  6.5 171.8 %all-reduce.4.cloned.1.call-start = ((), (), s32[]{:S(2)}) async-start(), calls=%async_computation | async-start | bytes 8388608 | tf_op jit(solution)/shard_map/psum | solution.py:70
  16.2 2.4 copy-start.6
  20.9 1.6 copy-start.3
  20.9 186.2 %all-gather.5.cloned.1.call-start = ((), (), s32[]{:S(2)}) async-start(), calls=%async_computation.2 | async-start | bytes 2621440 | tf_op jit(solution)/shard_map/all_gather | solution.py:13
  180.7 2.2 copy-start
  180.7 2.8 slice-start
  185.4 106.6 %all-reduce.6.cloned.1.call-start = ((), (), s32[]{:S(2)}) async-start(), calls=%async_computation.1 | async-start | bytes 2097152 | tf_op jit(solution)/shard_map/psum | solution.py:86
  188.1 2.4 copy-start.7
  190.1 104.1 %copy-start.4 = (f32[256,256]{1,0:T(8,128)}, f32[256,256]{1,0:T(8,128)S(1)}, u32[]{:S(2)}) copy-start(f32[256,256]{1,0:T(8,128)S(1)} %get-tuple-element.15) | copy-start | bytes 786436
  190.1 104.1 %copy-start.5 = (f32[256,256]{1,0:T(8,128)}, f32[256,256]{1,0:T(8,128)S(1)}, u32[]{:S(2)}) copy-start(f32[256,256]{1,0:T(8,128)S(1)} %get-tuple-element.16) | copy-start | bytes 786436
  213.6 3.3 %copy-start.1 = (bf16[4096,512]{1,0:T(8,128)(2,1)S(1)}, bf16[4096,512]{1,0:T(8,128)(2,1)}, u32[]{:S(2)}) copy-start(bf16[4096,512]{1,0:T(8,128)(2,1)} %all-reduce.4.cloned.1.call-done) | copy-start | bytes 12582916
  297.2 3.1 copy-start.8
  298.6 1.7 copy-start.10
  298.6 2.5 copy-start.2
  298.6 2.5 copy-start.9
Sparse Core Ops, SparseCore 0:
  21.1 157.1 all-reduce.3
  185.6 21.5 all-gather.4
  213.7 78.2 all-reduce.5
